TPU v7x, 32 devices: a whole 2x2x4 slice. The times are simulated.
32 devices in a mesh: dp: 4 (over z), shard: 8 (over y, x, core).
Axes of the slice: x: 2, y: 2, z: 4, core: 2. Of those that a mesh axis runs over, the one named last changes fastest.
Arguments:
- gradients: bfloat16 [4, 2, 512, 16, 512], P('dp', None, 'shard'), may hold values from -6 to 6
- owner_list: int32 [32], replicated, may hold values from 0 to 31, as said below
- row_offset: int32 [32], replicated, may hold values from 0 to 512, as said below
- col_offset: int32 [32], replicated, may hold values from 0 to 7680, as said below
- left_factor: float32 [64, 512, 512], P(('dp', 'shard')), may hold values from -32 to 32, as said below
- right_factor: float32 [64, 512, 512], P(('dp', 'shard')), may hold values from -32 to 32, as said below
- left_root: float32 [64, 512, 512], P(('dp', 'shard')), may hold values from -2 to 2, as said below
- right_root: float32 [64, 512, 512], P(('dp', 'shard')), may hold values from -2 to 2, as said below
Outputs:
- update: bfloat16 [2, 512, 16, 512], P(None, 'shard', None, 'dp')
- new_left_factor: float32 [64, 512, 512], P(('dp', 'shard'))
- new_right_factor: float32 [64, 512, 512], P(('dp', 'shard'))
- new_left_root: float32 [64, 512, 512], P(('dp', 'shard'))
- new_right_root: float32 [64, 512, 512], P(('dp', 'shard'))
Inputs may be any that keep to these rules, and one draw needn't show every extreme that they name: `owner_list`: no owner is named by more than 2 entries, and some owner by exactly 2. `row_offset`: multiples of 512; with col_offset, every block of the 2 x 16 grid is named exactly once. `col_offset`: multiples of 512; with row_offset, every block of the grid is named exactly once. `left_factor`: each slot symmetric positive definite. `right_factor`: each slot symmetric positive definite. `left_root`: each slot symmetric. `right_root`: each slot symmetric.
All inputs are finite; a program needn't handle non-finite values.
Results may differ from a plain program's by a relative error of at most 0.012.
Values may be sent and summed in bfloat16 or wider, within the bound.
A program may use at most 128 MiB of HBM per device.

v0:
```python
import functools

import jax
import jax.numpy as jnp
from jax import lax
from jax.experimental import pallas as pl
from jax.experimental.pallas import tpu as pltpu
from jax.sharding import PartitionSpec as P

decay_rate = 0.9
MESH = pl.DeviceIdType.MESH
f32 = jnp.float32
bf16 = jnp.bfloat16


def split(x):
    hi = x.astype(bf16)
    return hi, (x - hi.astype(f32)).astype(bf16)


def mm(a, b, ca=1, cb=0):
    return lax.dot_general(a, b, (((ca,), (cb,)), ((), ())), preferred_element_type=f32)


def mm3(a, b):
    return mm(a[0], b[0]) + (mm(a[0], b[1]) + mm(a[1], b[0]))


def reduce_kernel(n, blk_ref, grad_ref, out_ref, own, from_left, from_right, acc, pieces,
                  load_sem, send_sem, left_sem, right_sem):
    me = lax.axis_index("dp")
    shard = lax.axis_index("shard")
    parts, rows, cols, width = own.shape[1:]
    loads = {}
    order = []
    for j in range(n):
        for t in (n - 1 - j, j):
            if t not in order:
                order.append(t)
    for t in order:
        for b in range(parts):
            loads[t, b] = pltpu.make_async_copy(
                grad_ref.at[0, b, :, :, pl.ds(t * width, width)], own.at[t, b], load_sem.at[t, b]
            )
            loads[t, b].start()
    barrier = pltpu.get_barrier_semaphore()

    @pl.when(me > 0)
    def _():
        pl.semaphore_signal(barrier, inc=1, device_id=(me - 1, shard), device_id_type=MESH)

    @pl.when(me < n - 1)
    def _():
        pl.semaphore_signal(barrier, inc=1, device_id=(me + 1, shard), device_id_type=MESH)

    peers = (me > 0).astype(jnp.int32) + (me < n - 1).astype(jnp.int32)
    pl.semaphore_wait(barrier, peers)

    for t in order:
        for b in range(parts):
            loads[t, b].wait()

    def hop(t, b, step):
        buffer, sem = (from_left, left_sem) if step > 0 else (from_right, right_sem)
        return pltpu.make_async_remote_copy(
            src_ref=own.at[t, b],
            dst_ref=buffer.at[t, b],
            send_sem=send_sem.at[t, b],
            recv_sem=sem.at[t, b],
            device_id=(me + step, shard),
            device_id_type=MESH,
        )

    def pass_on(t, b, step):
        inner = me > 0 if step > 0 else me < n - 1
        buffer = from_left if step > 0 else from_right

        @pl.when(inner)
        def _():
            hop(t, b, step).wait_recv()
            own[t, b] = (own[t, b].astype(f32) + buffer[t, b].astype(f32)).astype(bf16)

        hop(t, b, step).start()

    for j in range(n - 1):
        for b in range(parts):
            for t, step in ((n - 1 - j, 1), (j, -1)):
                pl.when(me < t if step > 0 else me > t)(
                    functools.partial(pass_on, t, b, step)
                )
    for b in range(parts):
        acc[b] = own[me, b].astype(f32)

        @pl.when(me > 0)
        def _():
            hop(me, b, 1).wait_recv()
            acc[b] += from_left[me, b].astype(f32)

        @pl.when(me < n - 1)
        def _():
            hop(me, b, -1).wait_recv()
            acc[b] += from_right[me, b].astype(f32)

        for c in range(cols):
            pieces[b * cols + c] = acc[b, :, c, :].astype(bf16)

    @pl.loop(0, out_ref.shape[0])
    def _(s):
        out_ref[s] = pieces[blk_ref[s]]

    for t in range(n):
        for b in range(parts):

            @pl.when(me != t)
            def _():
                hop(t, b, 1).wait_send()


def power_kernel(left_ref, right_ref, lh_ref, ll_ref, rh_ref, rl_ref):
    for x_ref, h_ref, l_ref in ((left_ref, lh_ref, ll_ref), (right_ref, rh_ref, rl_ref)):
        x = split(x_ref[0])
        square = split(mm3(x, x))
        quad = split(mm3(square, square))
        hi, lo = split(mm3(quad, x))
        h_ref[0] = hi
        l_ref[0] = lo


def root_of(factor, power, old_root):
    size = factor.shape[0]
    row = lax.broadcasted_iota(jnp.int32, factor.shape, 0)
    col = lax.broadcasted_iota(jnp.int32, factor.shape, 1)
    trace = jnp.sum(jnp.where(row == col, factor, 0.0))
    return 1.25 * old_root - mm3(power, split(factor)) * (size / (4.0 * trace))


def step_kernel(dp, sh, slots, count_ref, in_ref, lf_ref, rf_ref, lr_ref, rr_ref, lh_ref, ll_ref,
                rh_ref, rl_ref, out_ref, nlf_ref, nrf_ref, nlr_ref, nrr_ref, g_ref):
    slot = pl.program_id(0)
    live = slot < count_ref[0]
    rows, width = in_ref.shape[1:]
    size = g_ref.shape[0]
    for d in range(dp):
        for s in range(sh):
            g_ref[s * rows:(s + 1) * rows, d * width:(d + 1) * width] = in_ref[
                (d * sh + s) * slots + slot
            ]
    g = g_ref[...]
    rate = (1.0 - decay_rate) / size
    left = decay_rate * lf_ref[0] + rate * mm(g, g, 1, 1)
    right = decay_rate * rf_ref[0] + rate * mm(g, g, 0, 0)
    nlf_ref[0] = jnp.where(live, left, lf_ref[0])
    nrf_ref[0] = jnp.where(live, right, rf_ref[0])
    left_root = root_of(left, (lh_ref[0], ll_ref[0]), lr_ref[0])
    nlr_ref[0] = jnp.where(live, left_root, lr_ref[0])
    right_root = root_of(right, (rh_ref[0], rl_ref[0]), rr_ref[0])
    nrr_ref[0] = jnp.where(live, right_root, rr_ref[0])
    hi, lo = split(left_root)
    product = split(mm(hi, g) + mm(lo, g))
    g_ref[...] = mm3(product, split(right_root)).astype(bf16)
    for d in range(dp):
        for s in range(sh):
            out_ref[(d * sh + s) * slots + slot] = g_ref[
                s * rows:(s + 1) * rows, d * width:(d + 1) * width
            ]


def place_kernel(slot_ref, in_ref, out_ref, acc):
    row_blocks, _, col_blocks, _ = out_ref.shape
    for b in range(row_blocks):
        for c in range(col_blocks):
            acc[b, :, c, :] = in_ref[slot_ref[b * col_blocks + c]].astype(f32)
        out_ref[b] = acc[b].astype(bf16)


def body(
    gradients, owner_list, row_offset, col_offset, left_factor, right_factor, left_root, right_root
):
    dp = lax.axis_size("dp")
    sh = lax.axis_size("shard")
    slots, size, _ = left_factor.shape
    _, parts, rows, cols, _ = gradients.shape
    width = size // dp
    total = dp * sh * slots
    blocks = owner_list.shape[0]
    block_at = row_offset // size * cols + col_offset // size
    entry_index = jnp.arange(blocks, dtype=jnp.int32)
    same_owner = owner_list[None, :] == owner_list[:, None]
    earlier = jnp.sum(same_owner & (entry_index[None, :] < entry_index[:, None]), axis=1)
    slot_of = owner_list * slots + earlier
    slot_index = jnp.arange(total, dtype=jnp.int32)
    block_of_slot = jnp.sum(
        jnp.where(slot_of[None, :] == slot_index[:, None], block_at[None, :], 0), axis=1
    ).astype(jnp.int32)
    slot_of_block = jnp.sum(
        jnp.where(block_at[None, :] == entry_index[:, None], slot_of[None, :], 0), axis=1
    ).astype(jnp.int32)
    my_index = lax.axis_index(("dp", "shard"))
    my_count = jnp.sum((owner_list == my_index).astype(jnp.int32), keepdims=True)

    smem = pl.BlockSpec(memory_space=pltpu.SMEM)
    vmem = pl.BlockSpec(memory_space=pltpu.VMEM)
    chunk = (dp, parts, rows, cols, width)
    sems = pltpu.SemaphoreType.DMA((dp, parts))
    outgoing = pl.pallas_call(
        functools.partial(reduce_kernel, dp),
        out_shape=jax.ShapeDtypeStruct((total, rows, width), bf16),
        in_specs=[smem, pl.BlockSpec(memory_space=pl.ANY)],
        out_specs=vmem,
        scratch_shapes=[
            pltpu.VMEM(chunk, bf16),
            pltpu.VMEM(chunk, bf16),
            pltpu.VMEM(chunk, bf16),
            pltpu.VMEM(chunk[1:], f32),
            pltpu.VMEM((parts * cols, rows, width), bf16),
            sems, sems, sems, sems,
        ],
        compiler_params=pltpu.CompilerParams(
            collective_id=0, has_side_effects=True, vmem_limit_bytes=48 * 2**20
        ),
        cost_estimate=pl.CostEstimate(flops=10**9, bytes_accessed=2**22, transcendentals=0),
        name="reduce_columns",
    )(block_of_slot, gradients)
    incoming = lax.all_to_all(outgoing, ("dp", "shard"), split_axis=0, concat_axis=0, tiled=True)

    matrix = pl.BlockSpec((1, size, size), lambda i: (i, 0, 0))
    half = jax.ShapeDtypeStruct((slots, size, size), bf16)
    full = jax.ShapeDtypeStruct((slots, size, size), f32)
    powers = pl.pallas_call(
        power_kernel,
        grid=(slots,),
        out_shape=[half] * 4,
        in_specs=[matrix] * 2,
        out_specs=[matrix] * 4,
        cost_estimate=pl.CostEstimate(
            flops=36 * slots * size**3, bytes_accessed=16 * slots * size**2, transcendentals=0
        ),
        name="fifth_powers",
    )(left_root, right_root)
    whole = pl.BlockSpec((total, rows, width), lambda i: (0, 0, 0))
    outbound, *news = pl.pallas_call(
        functools.partial(step_kernel, dp, sh, slots),
        grid=(slots,),
        out_shape=[jax.ShapeDtypeStruct((total, rows, width), bf16)] + [full] * 4,
        in_specs=[smem, whole] + [matrix] * 8,
        out_specs=[whole] + [matrix] * 4,
        scratch_shapes=[pltpu.VMEM((size, size), bf16)],
        compiler_params=pltpu.CompilerParams(vmem_limit_bytes=56 * 2**20),
        name="step",
    )(my_count, incoming, left_factor, right_factor, left_root, right_root, *powers)
    returned = lax.all_to_all(outbound, ("dp", "shard"), split_axis=0, concat_axis=0, tiled=True)
    update = pl.pallas_call(
        place_kernel,
        out_shape=jax.ShapeDtypeStruct((parts, rows, cols, width), bf16),
        in_specs=[smem, vmem],
        out_specs=vmem,
        scratch_shapes=[pltpu.VMEM((parts, rows, cols, width), f32)],
        name="place",
    )(slot_of_block, returned)
    return (update, *news)


def solution(mesh):
    owned = P(("dp", "shard"), None, None)
    in_specs = (P("dp", None, "shard", None, None), P(), P(), P(), owned, owned, owned, owned)
    out_specs = (P(None, "shard", None, "dp"), owned, owned, owned, owned)
    return jax.shard_map(body, mesh=mesh, in_specs=in_specs, out_specs=out_specs, check_vma=False)
```

profile of v0, /device:TPU:9, one launch (start us, length us, event | category | flops | bytes accessed | tf_op | source)
XLA Modules:
  0.0 128.6 jit_solution(7174102407898032596)
XLA Ops:
  0.6 0.9 convert_reduce_fusion
  1.6 1.3 %fusion.1 = (s32[]{:T(128)}, s32[32]{0:T(128)S(1)}, s32[32]{0:T(128)S(1)}) fusion(s32[32]{0:T(128)} %param.9, s32[]{:T(128)S(6)} %add.13, s32[32]{0:T(128)S(1)} %convert_reduce_fusion, s32[32]{0:T(128)} %param.11, s32[32]{0:T(128)} %param.10), kind=kLoop, calls=%fused_computation.16 | loop fusion | flops 1183 | bytes 776 | tf_op jit(solution)/shard_map/reduce_sum | solution.py:199
  2.9 0.1 select_reduce_fusion.blk_ref
  3.0 0.0 copy-start
  3.0 1.6 %copy-done = bf16[1,2,64,16,512]{4,3,2,1,0:T(8,128)(2,1)S(1)} copy-done((bf16[1,2,64,16,512]{4,3,2,1,0:T(8,128)(2,1)S(1)}, bf16[1,2,64,16,512]{4,3,2,1,0:T(8,128)(2,1)}, u32[]{:S(2)}) %copy-start) | copy-done | bytes 2097176
  4.6 39.4 %reduce_columns.1 = bf16[64,64,128]{2,1,0:T(8,128)(2,1)} custom-call(s32[64]{0:T(128)S(1)} %select_reduce_fusion.blk_ref, bf16[1,2,64,16,512]{4,3,2,1,0:T(8,128)(2,1)S(1)} %copy-done), custom_call_target="tpu_custom_call" | custom-call | flops 1000000000 | bytes 4194304 | tf_op jit(solution)/shard_map/reduce_columns/pallas_call | solution.py:205
  44.0 10.7 %all-to-all-start = ((bf16[64,64,128]{2,1,0:T(8,128)(2,1)}), bf16[64,64,128]{2,1,0:T(8,128)(2,1)S(1)}, u32[]{:S(2)}, u32[]{:S(2)}) async-start(bf16[64,64,128]{2,1,0:T(8,128)(2,1)} %reduce_columns.1), calls=%async_computation | async-start | bytes 2097152 | tf_op jit(solution)/shard_map/all_to_all | solution.py:224
  54.7 13.0 %fifth_powers.1 = (bf16[2,512,512]{2,1,0:T(8,128)(2,1)}, bf16[2,512,512]{2,1,0:T(8,128)(2,1)}, bf16[2,512,512]{2,1,0:T(8,128)(2,1)}, bf16[2,512,512]{2,1,0:T(8,128)(2,1)}) custom-call(f32[2,512,512]{2,1,0:T(8,128)} %lr_ref.1, f32[2,512,512]{2,1,0:T(8,128)} %rr_ref.1), custom_call_target="tpu_custom_call" | custom-call | flops 9663676416 | bytes 8388608 | tf_op jit(solution)/shard_map/fifth_powers/pallas_call | solution.py:229
  67.7 12.3 %all-to-all-done.in_ref = bf16[64,64,128]{2,1,0:T(8,128)(2,1)S(1)} async-done(((bf16[64,64,128]{2,1,0:T(8,128)(2,1)}), bf16[64,64,128]{2,1,0:T(8,128)(2,1)S(1)}, u32[]{:S(2)}, u32[]{:S(2)}) %all-to-all-start) | async-done | bytes 1048608 | tf_op jit(solution)/shard_map/all_to_all | solution.py:224
  80.0 0.0 copy-start.2
  80.0 1.0 copy-done.2
  81.0 14.0 %step.1 = (bf16[64,64,128]{2,1,0:T(8,128)(2,1)}, f32[2,512,512]{2,1,0:T(8,128)}, f32[2,512,512]{2,1,0:T(8,128)}, f32[2,512,512]{2,1,0:T(8,128)}, f32[2,512,512]{2,1,0:T(8,128)}) custom-call(s32[1]{0:T(128)} %bitcast.count_ref, bf16[64,64,128]{2,1,0:T(8,128)(2,1)} %copy-done.2, f32[2,512,512]{2,1,0:T(8,128)} %lf_ref.1, f32[2,512,512]{2,1,0:T(8,128)} %rf_ref.1, ...), custom_call_target="tpu_custom_call" | custom-call | tf_op jit(solution)/shard_map/step/pallas_call | solution.py:241
  95.0 4.5 %all-to-all-start.1 = ((bf16[64,64,128]{2,1,0:T(8,128)(2,1)}), bf16[64,64,128]{2,1,0:T(8,128)(2,1)S(1)}, u32[]{:S(2)}, u32[]{:S(2)}) async-start(bf16[64,64,128]{2,1,0:T(8,128)(2,1)} %get-tuple-element.18), calls=%async_computation.1 | async-start | bytes 2097152 | tf_op jit(solution)/shard_map/all_to_all | solution.py:251
  99.5 0.7 select_reduce_fusion.1.slot_ref
  100.2 24.6 %all-to-all-done.1.in_ref = bf16[64,64,128]{2,1,0:T(8,128)(2,1)S(1)} async-done(((bf16[64,64,128]{2,1,0:T(8,128)(2,1)}), bf16[64,64,128]{2,1,0:T(8,128)(2,1)S(1)}, u32[]{:S(2)}, u32[]{:S(2)}) %all-to-all-start.1) | async-done | bytes 1048608 | tf_op jit(solution)/shard_map/all_to_all | solution.py:251
  124.8 0.0 copy-start.1
  124.8 1.0 copy-done.1
  125.8 2.8 %place.1 = bf16[2,64,16,128]{3,2,1,0:T(8,128)(2,1)} custom-call(s32[32]{0:T(128)} %select_reduce_fusion.1.slot_ref, bf16[64,64,128]{2,1,0:T(8,128)(2,1)} %copy-done.1), custom_call_target="tpu_custom_call" | custom-call | tf_op jit(solution)/shard_map/place/pallas_call | solution.py:252
Async XLA Ops:
  3.0 1.6 %copy-start = (bf16[1,2,64,16,512]{4,3,2,1,0:T(8,128)(2,1)S(1)}, bf16[1,2,64,16,512]{4,3,2,1,0:T(8,128)(2,1)}, u32[]{:S(2)}) copy-start(bf16[1,2,64,16,512]{4,3,2,1,0:T(8,128)(2,1)} %grad_ref.1) | copy-start | bytes 6291460
  44.0 36.0 %all-to-all-start = ((bf16[64,64,128]{2,1,0:T(8,128)(2,1)}), bf16[64,64,128]{2,1,0:T(8,128)(2,1)S(1)}, u32[]{:S(2)}, u32[]{:S(2)}) async-start(bf16[64,64,128]{2,1,0:T(8,128)(2,1)} %reduce_columns.1), calls=%async_computation | async-start | bytes 2097152 | tf_op jit(solution)/shard_map/all_to_all | solution.py:224
  80.0 1.0 copy-start.2
  95.0 29.8 %all-to-all-start.1 = ((bf16[64,64,128]{2,1,0:T(8,128)(2,1)}), bf16[64,64,128]{2,1,0:T(8,128)(2,1)S(1)}, u32[]{:S(2)}, u32[]{:S(2)}) async-start(bf16[64,64,128]{2,1,0:T(8,128)(2,1)} %get-tuple-element.18), calls=%async_computation.1 | async-start | bytes 2097152 | tf_op jit(solution)/shard_map/all_to_all | solution.py:251
  124.8 1.0 copy-start.1
where the time goes:
time: 131 us; the launch traced here: 129 us
  Pallas kernels  69.2 us (53%)
  waiting for transfers between devices  36.9 us (28%)
  starting transfers between devices  15.3 us (12%)
  local copies, waits for them, and re-layouts  3.59 us (3%)
  other arithmetic  3.04 us (2%)
    pallas_call x1, Pallas kernels, body(): pl.pallas_call(functools.partial(reduce_kernel, dp), out_shape=jax.ShapeD...  39.4 us
    all_to_all x1, waiting for transfers between devices, body(): lax.all_to_all(outbound, ('dp', 'shard'), split_axis=0, concat_axis=0, ti...  24.6 us
    pallas_call x1, Pallas kernels, body(): pl.pallas_call(functools.partial(step_kernel, dp, sh, slots), grid=(slots...  14 us
    pallas_call x1, Pallas kernels, body(): pl.pallas_call(power_kernel, grid=(slots,), out_shape=[half] * 4, in_spec...  13 us
    all_to_all x1, waiting for transfers between devices, body(): lax.all_to_all(outgoing, ('dp', 'shard'), split_axis=0, concat_axis=0, ti...  12.3 us
    all_to_all x1, starting transfers between devices, body(): lax.all_to_all(outgoing, ('dp', 'shard'), split_axis=0, concat_axis=0, ti...  10.7 us
    all_to_all x1, starting transfers between devices, body(): lax.all_to_all(outbound, ('dp', 'shard'), split_axis=0, concat_axis=0, ti...  4.54 us
    unnamed x6, local copies, waits for them, and re-layouts  3.59 us
  transfers between devices with their start and end apart: 2, of which 2 were waited for; matrix products, arithmetic and copies ran while one was open for 1% of the time, Pallas kernels for 10%

commit v1 on v0

v1 whole, which is shorter than its diff:
```python
import functools

import jax
import jax.numpy as jnp
from jax import lax
from jax.experimental import pallas as pl
from jax.experimental.pallas import tpu as pltpu
from jax.sharding import PartitionSpec as P

decay_rate = 0.9
MESH = pl.DeviceIdType.MESH
f32 = jnp.float32
bf16 = jnp.bfloat16


def split(x):
    hi = x.astype(bf16)
    return hi, (x - hi.astype(f32)).astype(bf16)


def mm(a, b, ca=1, cb=0):
    return lax.dot_general(a, b, (((ca,), (cb,)), ((), ())), preferred_element_type=f32)


def mm3(a, b):
    return mm(a[0], b[0]) + (mm(a[0], b[1]) + mm(a[1], b[0]))


def fifth_power(x):
    x = split(x)
    square = split(mm3(x, x))
    quad = split(mm3(square, square))
    return split(mm3(quad, x))


def root_of(factor, power, old_root):
    size = factor.shape[0]
    row = lax.broadcasted_iota(jnp.int32, factor.shape, 0)
    col = lax.broadcasted_iota(jnp.int32, factor.shape, 1)
    trace = jnp.sum(jnp.where(row == col, factor, 0.0))
    return 1.25 * old_root - mm3(power, split(factor)) * (size / (4.0 * trace))


def shampoo_kernel(n, sh, slots, table_ref, grad_ref, lf_hbm, rf_hbm, lr_hbm, rr_hbm,
                   out_ref, nlf_ref, nrf_ref, nlr_ref, nrr_ref,
                   own, from_left, from_right, acc, pieces, packed, g_ref, u_ref, returned,
                   factors, roots, powers,
                   load_sem, factor_sem, root_sem, send_sem, left_sem, right_sem,
                   out_sem, in_sem, back_out_sem, back_in_sem):
    me = lax.axis_index("dp")
    shard = lax.axis_index("shard")
    total = n * sh
    parts, rows, cols, width = own.shape[1:]
    size = g_ref.shape[1]
    blocks = parts * cols
    index = me * sh + shard
    loads = {}
    order = []
    for j in range(n):
        for t in (n - 1 - j, j):
            if t not in order:
                order.append(t)
    for t in order:
        for b in range(parts):
            loads[t, b] = pltpu.make_async_copy(
                grad_ref.at[0, b, :, :, pl.ds(t * width, width)], own.at[t, b], load_sem.at[t, b]
            )
            loads[t, b].start()
    root_loads = [
        pltpu.make_async_copy(ref, roots.at[i], root_sem.at[i])
        for i, ref in enumerate((lr_hbm, rr_hbm))
    ]
    factor_loads = [
        pltpu.make_async_copy(ref, factors.at[i], factor_sem.at[i])
        for i, ref in enumerate((lf_hbm, rf_hbm))
    ]
    for copy in root_loads + factor_loads:
        copy.start()
    barrier = pltpu.get_barrier_semaphore()

    @pl.loop(1, total)
    def _(r):
        to = lax.rem(index + r, total)
        pl.semaphore_signal(
            barrier, inc=1, device_id=(to // sh, lax.rem(to, sh)), device_id_type=MESH
        )

    for t in order:
        for b in range(parts):
            loads[t, b].wait()
    pl.semaphore_wait(barrier, total - 1)

    def hop(t, b, step):
        buffer, sem = (from_left, left_sem) if step > 0 else (from_right, right_sem)
        return pltpu.make_async_remote_copy(
            src_ref=own.at[t, b],
            dst_ref=buffer.at[t, b],
            send_sem=send_sem.at[t, b],
            recv_sem=sem.at[t, b],
            device_id=(me + step, shard),
            device_id_type=MESH,
        )

    units = [(i, s) for s in range(slots) for i in range(2)]

    def next_power():
        if units:
            i, s = units.pop(0)
            hi, lo = fifth_power(roots[i, s])
            powers[i, 0, s] = hi
            powers[i, 1, s] = lo

    def first_hop(t, b, step):
        hop(t, b, step).start()

    def pass_on(t, b, step):
        hop(t, b, step).wait_recv()
        buffer = from_left if step > 0 else from_right
        own[t, b] = (own[t, b].astype(f32) + buffer[t, b].astype(f32)).astype(bf16)
        hop(t, b, step).start()

    hops = [
        (t, b, step)
        for j in range(n - 1)
        for b in range(parts)
        for t, step in ((n - 1 - j, 1), (j, -1))
    ]
    for t, b, step in hops:
        pl.when(me == (0 if step > 0 else n - 1))(functools.partial(first_hop, t, b, step))
    for copy in root_loads:
        copy.wait()
    next_power()
    every = max(1, 2 * parts // 2)
    for k, (t, b, step) in enumerate(hops):
        inner = (me < t) & (me > 0) if step > 0 else (me > t) & (me < n - 1)
        pl.when(inner)(functools.partial(pass_on, t, b, step))
        if k % every == every - 1:
            next_power()
    while units:
        next_power()
    for copy in factor_loads:
        copy.wait()
    for b in range(parts):
        acc[b] = own[me, b].astype(f32)

        @pl.when(me > 0)
        def _():
            hop(me, b, 1).wait_recv()
            acc[b] += from_left[me, b].astype(f32)

        @pl.when(me < n - 1)
        def _():
            hop(me, b, -1).wait_recv()
            acc[b] += from_right[me, b].astype(f32)

        for c in range(cols):
            pieces[b * cols + c] = acc[b, :, c, :].astype(bf16)

    my_rows = pl.ds(pl.multiple_of(shard * rows, rows), rows)
    my_cols = pl.ds(pl.multiple_of(me * width, width), width)

    def peers(visit):
        for dz in sorted(range(n), key=lambda d: abs(2 * d - n)):
            @pl.loop(0 if dz else 1, sh)
            def _(ds):
                visit(lax.rem(me + dz, n), lax.rem(shard + ds, sh))

    def forward(slot):
        @pl.loop(0, total)
        def _(d):
            packed[slot, d] = pieces[table_ref[d * slots + slot]]

        def send(z, s):
            pltpu.make_async_remote_copy(
                src_ref=packed.at[slot, z * sh + s],
                dst_ref=g_ref.at[slot, my_rows, my_cols],
                send_sem=out_sem.at[slot],
                recv_sem=in_sem.at[slot],
                device_id=(z, s),
                device_id_type=MESH,
            ).start()

        peers(send)
        g_ref[slot, my_rows, my_cols] = packed[slot, index]

    def backward(slot):
        def send(z, s):
            pltpu.make_async_remote_copy(
                src_ref=u_ref.at[
                    slot,
                    pl.ds(pl.multiple_of(s * rows, rows), rows),
                    pl.ds(pl.multiple_of(z * width, width), width),
                ],
                dst_ref=returned.at[index * slots + slot],
                send_sem=back_out_sem.at[slot],
                recv_sem=back_in_sem.at[slot],
                device_id=(z, s),
                device_id_type=MESH,
            ).start()

        peers(send)
        returned[index * slots + slot] = u_ref[slot, my_rows, my_cols]

    def wait_all(sem):
        ref = packed.at[0, pl.ds(0, total - 1)]
        pltpu.make_async_copy(ref, ref, sem).wait()

    count = table_ref[total * slots + blocks]
    rate = (1.0 - decay_rate) / size

    def step(slot):
        live = slot < count
        g = g_ref[slot]
        left_old, right_old = factors[0, slot], factors[1, slot]
        left = decay_rate * left_old + rate * mm(g, g, 1, 1)
        right = decay_rate * right_old + rate * mm(g, g, 0, 0)
        nlf_ref[slot] = jnp.where(live, left, left_old)
        nrf_ref[slot] = jnp.where(live, right, right_old)
        left_root = root_of(left, (powers[0, 0, slot], powers[0, 1, slot]), roots[0, slot])
        nlr_ref[slot] = jnp.where(live, left_root, roots[0, slot])
        right_root = root_of(right, (powers[1, 0, slot], powers[1, 1, slot]), roots[1, slot])
        nrr_ref[slot] = jnp.where(live, right_root, roots[1, slot])
        hi, lo = split(left_root)
        product = split(mm(hi, g) + mm(lo, g))
        u_ref[slot] = mm3(product, split(right_root)).astype(bf16)

    for slot in range(slots):
        forward(slot)
    for slot in range(slots):
        wait_all(in_sem.at[slot])
        step(slot)
        backward(slot)
    for slot in range(slots):
        wait_all(back_in_sem.at[slot])
    for b in range(parts):
        for c in range(cols):
            acc[b, :, c, :] = returned[table_ref[total * slots + b * cols + c]].astype(f32)
        out_ref[b] = acc[b].astype(bf16)
    for slot in range(slots):
        wait_all(out_sem.at[slot])
        wait_all(back_out_sem.at[slot])
    for t in range(n):
        for b in range(parts):

            @pl.when(me != t)
            def _():
                hop(t, b, 1).wait_send()


def body(
    gradients, owner_list, row_offset, col_offset, left_factor, right_factor, left_root, right_root
):
    dp = lax.axis_size("dp")
    sh = lax.axis_size("shard")
    slots, size, _ = left_factor.shape
    _, parts, rows, cols, _ = gradients.shape
    width = size // dp
    total = dp * sh
    blocks = owner_list.shape[0]
    block_at = row_offset // size * cols + col_offset // size
    entry_index = jnp.arange(blocks, dtype=jnp.int32)
    same_owner = owner_list[None, :] == owner_list[:, None]
    earlier = jnp.sum(same_owner & (entry_index[None, :] < entry_index[:, None]), axis=1)
    slot_of = owner_list * slots + earlier
    slot_index = jnp.arange(total * slots, dtype=jnp.int32)
    block_of_slot = jnp.sum(
        jnp.where(slot_of[None, :] == slot_index[:, None], block_at[None, :], 0), axis=1
    )
    slot_of_block = jnp.sum(
        jnp.where(block_at[None, :] == entry_index[:, None], slot_of[None, :], 0), axis=1
    )
    my_index = lax.axis_index(("dp", "shard"))
    my_count = jnp.sum((owner_list == my_index).astype(jnp.int32), keepdims=True)
    table = jnp.concatenate([block_of_slot, slot_of_block, my_count]).astype(jnp.int32)

    smem = pl.BlockSpec(memory_space=pltpu.SMEM)
    vmem = pl.BlockSpec(memory_space=pltpu.VMEM)
    hbm = pl.BlockSpec(memory_space=pl.ANY)
    chunk = (dp, parts, rows, cols, width)
    matrices = (slots, size, size)
    dma = pltpu.SemaphoreType.DMA
    full = jax.ShapeDtypeStruct(matrices, f32)
    return pl.pallas_call(
        functools.partial(shampoo_kernel, dp, sh, slots),
        out_shape=[jax.ShapeDtypeStruct((parts, rows, cols, width), bf16)] + [full] * 4,
        in_specs=[smem] + [hbm] * 5,
        out_specs=[vmem] * 5,
        scratch_shapes=[
            pltpu.VMEM(chunk, bf16),
            pltpu.VMEM(chunk, bf16),
            pltpu.VMEM(chunk, bf16),
            pltpu.VMEM(chunk[1:], f32),
            pltpu.VMEM((parts * cols, rows, width), bf16),
            pltpu.VMEM((slots, total, rows, width), bf16),
            pltpu.VMEM(matrices, bf16),
            pltpu.VMEM(matrices, bf16),
            pltpu.VMEM((total * slots, rows, width), bf16),
            pltpu.VMEM((2,) + matrices, f32),
            pltpu.VMEM((2,) + matrices, f32),
            pltpu.VMEM((2, 2) + matrices, bf16),
            dma((dp, parts)), dma((2,)), dma((2,)),
            dma((dp, parts)), dma((dp, parts)), dma((dp, parts)),
            dma((slots,)), dma((slots,)), dma((slots,)), dma((slots,)),
        ],
        compiler_params=pltpu.CompilerParams(
            collective_id=0, has_side_effects=True, vmem_limit_bytes=60 * 2**20
        ),
        name="shampoo",
    )(table, gradients, left_factor, right_factor, left_root, right_root)


def solution(mesh):
    owned = P(("dp", "shard"), None, None)
    in_specs = (P("dp", None, "shard", None, None), P(), P(), P(), owned, owned, owned, owned)
    out_specs = (P(None, "shard", None, "dp"), owned, owned, owned, owned)
    return jax.shard_map(body, mesh=mesh, in_specs=in_specs, out_specs=out_specs, check_vma=False)
```

time: 131 us -> 124 us (0.947); the launches traced: 129 us -> 123 us
  Pallas kernels: 69.2 us -> 108 us
  waiting for transfers between devices: 36.9 us -> 0 us
  starting transfers between devices: 15.3 us -> 0 us
  local copies, waits for them, and re-layouts: 3.59 us -> 11.1 us
    pallas_call x4 -> x1, Pallas kernels: 69.2 us -> 108 us  [body(): pl.pallas_call(functools.partial(shampoo_kernel, dp, sh, slots), out_shap...]
    all_to_all x2 -> x0, waiting for transfers between devices: 36.9 us -> none  [the longest x1 24.6 us: body(): lax.all_to_all(outbound, ('dp', 'shard'), split_axis=0, concat_axis=0, ti...]
    all_to_all x2 -> x0, starting transfers between devices: 15.3 us -> none  [the longest x1 10.7 us: body(): lax.all_to_all(outgoing, ('dp', 'shard'), split_axis=0, concat_axis=0, ti...]
    unnamed x6 -> x11, local copies, waits for them, and re-layouts: 3.59 us -> 11.1 us
    add x0 -> x1, other arithmetic: none -> 1.33 us  [body(): slot_of = owner_list * slots + earlier]
    reduce_sum x1 -> x0, other arithmetic: 1.33 us -> none  [body(): jnp.sum((owner_list == my_index).astype(jnp.int32), keepdims=True)]
  transfers between devices with their start and end apart: 2 -> 0, of which waited for: 2 -> 0; matrix products, arithmetic and copies ran while one was open for 1% -> 0% of each run, Pallas kernels for 10% -> 0%
where the time goes in v1:
time: 124 us; the launch traced here: 123 us
  Pallas kernels  108 us (87%)
  local copies, waits for them, and re-layouts  11.1 us (9%)
  other arithmetic  3.68 us (3%)
    pallas_call x1, Pallas kernels, body(): pl.pallas_call(functools.partial(shampoo_kernel, dp, sh, slots), out_shap...  108 us
    unnamed x11, local copies, waits for them, and re-layouts  11.1 us

profile of v1, /device:TPU:9, one launch (start us, length us, event | category | flops | bytes accessed | tf_op | source)
XLA Modules:
  0.0 123.4 jit_solution(17068384276469474441)
XLA Ops:
  0.6 0.9 convert_reduce_fusion
  1.5 1.3 %multiply_add_fusion = (s32[32]{0:T(128)S(1)}, s32[]{:T(128)}, s32[32]{0:T(128)S(1)}) fusion(s32[32]{0:T(128)S(1)} %convert_reduce_fusion, s32[32]{0:T(128)} %param.9, s32[]{:T(128)S(6)} %add.13, s32[32]{0:T(128)} %param.11, s32[32]{0:T(128)} %param.10), kind=kLoop, calls=%fused_computation.19 | loop fusion | flops 1183 | bytes 776 | tf_op jit(solution)/shard_map/add | solution.py:264
  2.9 0.1 select_reduce_fusion
  3.0 0.1 select_reduce_fusion.1
  3.1 1.2 %pad_add_fusion.table_ref = s32[97]{0:T(128)} fusion(s32[1]{0:T(128)} %bitcast, s32[32]{0:T(128)S(1)} %select_reduce_fusion, s32[64]{0:T(128)S(1)} %select_reduce_fusion.1), kind=kLoop, calls=%fused_computation.17 | loop fusion | flops 194 | bytes 776 | tf_op jit(solution)/shard_map/concatenate | solution.py:274
  4.3 108.0 %shampoo.1 = (bf16[2,64,16,128]{3,2,1,0:T(8,128)(2,1)}, f32[2,512,512]{2,1,0:T(8,128)}, f32[2,512,512]{2,1,0:T(8,128)}, f32[2,512,512]{2,1,0:T(8,128)}, f32[2,512,512]{2,1,0:T(8,128)}) custom-call(s32[97]{0:T(128)} %pad_add_fusion.table_ref, bf16[1,2,64,16,512]{4,3,2,1,0:T(8,128)(2,1)} %grad_ref.1, f32[2,512,512]{2,1,0:T(8,128)} %lf_hbm.1, ...), custom_call_target="tpu_custom_call" | custom-call | tf_op jit(solution)/shard_map/shampoo/pallas_call | solution.py:283
  112.3 1.9 %copy.18 = bf16[2,64,16,128]{3,2,1,0:T(8,128)(2,1)} copy(bf16[2,64,16,128]{3,2,1,0:T(8,128)(2,1)} %get-tuple-element.13) | data formatting | bytes 1048576
  114.2 0.0 copy-start.2
  114.2 3.2 %copy.19 = f32[2,512,512]{2,1,0:T(8,128)} copy(f32[2,512,512]{2,1,0:T(8,128)} %get-tuple-element.14) | data formatting | bytes 4194304
  117.4 0.0 copy-done.2
  117.4 0.0 copy-start.1
  117.4 1.3 %copy.20 = f32[2,512,512]{2,1,0:T(8,128)} copy(f32[2,512,512]{2,1,0:T(8,128)S(1)} %copy-done.2) | data formatting | bytes 4194304
  118.7 1.0 copy-done.1
  119.8 0.0 copy-start
  119.8 1.3 %copy.21 = f32[2,512,512]{2,1,0:T(8,128)} copy(f32[2,512,512]{2,1,0:T(8,128)S(1)} %copy-done.1) | data formatting | bytes 4194304
  121.1 1.0 copy-done
  122.1 1.3 %copy.22 = f32[2,512,512]{2,1,0:T(8,128)} copy(f32[2,512,512]{2,1,0:T(8,128)S(1)} %copy-done) | data formatting | bytes 4194304
Async XLA Ops:
  114.2 3.2 %copy-start.2 = (f32[2,512,512]{2,1,0:T(8,128)S(1)}, f32[2,512,512]{2,1,0:T(8,128)}, u32[]{:S(2)}) copy-start(f32[2,512,512]{2,1,0:T(8,128)} %get-tuple-element.15) | copy-start | bytes 6291460
  117.4 2.3 %copy-start.1 = (f32[2,512,512]{2,1,0:T(8,128)S(1)}, f32[2,512,512]{2,1,0:T(8,128)}, u32[]{:S(2)}) copy-start(f32[2,512,512]{2,1,0:T(8,128)} %get-tuple-element.16) | copy-start | bytes 6291460
  119.8 2.3 %copy-start = (f32[2,512,512]{2,1,0:T(8,128)S(1)}, f32[2,512,512]{2,1,0:T(8,128)}, u32[]{:S(2)}) copy-start(f32[2,512,512]{2,1,0:T(8,128)} %get-tuple-element.17) | copy-start | bytes 6291460

commit v2 on v1

--- a/solution.py
+++ b/solution.py
@@ -42,8 +42,8 @@
 
 
 def shampoo_kernel(n, sh, slots, table_ref, grad_ref, lf_hbm, rf_hbm, lr_hbm, rr_hbm,
-                   out_ref, nlf_ref, nrf_ref, nlr_ref, nrr_ref,
-                   own, from_left, from_right, acc, pieces, packed, g_ref, u_ref, returned,
+                   returned, nlf_ref, nrf_ref, nlr_ref, nrr_ref,
+                   own, from_left, from_right, acc, pieces, packed, g_ref, u_ref,
                    factors, roots, powers,
                    load_sem, factor_sem, root_sem, send_sem, left_sem, right_sem,
                    out_sem, in_sem, back_out_sem, back_in_sem):
@@ -232,10 +232,6 @@
         backward(slot)
     for slot in range(slots):
         wait_all(back_in_sem.at[slot])
-    for b in range(parts):
-        for c in range(cols):
-            acc[b, :, c, :] = returned[table_ref[total * slots + b * cols + c]].astype(f32)
-        out_ref[b] = acc[b].astype(bf16)
     for slot in range(slots):
         wait_all(out_sem.at[slot])
         wait_all(back_out_sem.at[slot])
@@ -245,6 +241,24 @@
             @pl.when(me != t)
             def _():
                 hop(t, b, 1).wait_send()
+
+
+def place_kernel(first, table_ref, returned, *refs):
+    news, out_ref, outs = refs[:4], refs[4], refs[5:9]
+    acc, sems = refs[9:]
+    copies = [
+        pltpu.make_async_copy(new, out, sems.at[i])
+        for i, (new, out) in enumerate(zip(news, outs))
+    ]
+    for copy in copies:
+        copy.start()
+    parts, _, cols, _ = out_ref.shape
+    for b in range(parts):
+        for c in range(cols):
+            acc[b, :, c, :] = returned[table_ref[first + b * cols + c]].astype(f32)
+        out_ref[b] = acc[b].astype(bf16)
+    for copy in copies:
+        copy.wait()
 
 
 def body(
@@ -275,14 +289,15 @@
 
     smem = pl.BlockSpec(memory_space=pltpu.SMEM)
     vmem = pl.BlockSpec(memory_space=pltpu.VMEM)
-    hbm = pl.BlockSpec(memory_space=pl.ANY)
+    hbm = pl.BlockSpec(memory_space=pltpu.HBM)
     chunk = (dp, parts, rows, cols, width)
     matrices = (slots, size, size)
     dma = pltpu.SemaphoreType.DMA
     full = jax.ShapeDtypeStruct(matrices, f32)
-    return pl.pallas_call(
+    pieces = (total * slots, rows, width)
+    returned, *news = pl.pallas_call(
         functools.partial(shampoo_kernel, dp, sh, slots),
-        out_shape=[jax.ShapeDtypeStruct((parts, rows, cols, width), bf16)] + [full] * 4,
+        out_shape=[pltpu.VMEM(pieces, bf16)] + [pltpu.VMEM(matrices, f32)] * 4,
         in_specs=[smem] + [hbm] * 5,
         out_specs=[vmem] * 5,
         scratch_shapes=[
@@ -294,7 +309,6 @@
             pltpu.VMEM((slots, total, rows, width), bf16),
             pltpu.VMEM(matrices, bf16),
             pltpu.VMEM(matrices, bf16),
-            pltpu.VMEM((total * slots, rows, width), bf16),
             pltpu.VMEM((2,) + matrices, f32),
             pltpu.VMEM((2,) + matrices, f32),
             pltpu.VMEM((2, 2) + matrices, bf16),
@@ -303,10 +317,19 @@
             dma((slots,)), dma((slots,)), dma((slots,)), dma((slots,)),
         ],
         compiler_params=pltpu.CompilerParams(
-            collective_id=0, has_side_effects=True, vmem_limit_bytes=60 * 2**20
+            collective_id=0, has_side_effects=True, vmem_limit_bytes=48 * 2**20
         ),
         name="shampoo",
     )(table, gradients, left_factor, right_factor, left_root, right_root)
+    return pl.pallas_call(
+        functools.partial(place_kernel, total * slots),
+        out_shape=[jax.ShapeDtypeStruct((parts, rows, cols, width), bf16)] + [full] * 4,
+        in_specs=[smem] + [vmem] * 5,
+        out_specs=[vmem] + [hbm] * 4,
+        scratch_shapes=[pltpu.VMEM((parts, rows, cols, width), f32), dma((4,))],
+        compiler_params=pltpu.CompilerParams(vmem_limit_bytes=16 * 2**20),
+        name="place",
+    )(table, returned, *news)
 
 
 def solution(mesh):

time: 124 us -> 113 us (0.911)
  local copies, waits for them, and re-layouts: 11.1 us -> 0.01 us
    unnamed x11 -> x2, local copies, waits for them, and re-layouts: 11.1 us -> 0.01 us
    pallas_call x0 -> x1, Pallas kernels: none -> 4.7 us  [body(): pl.pallas_call(functools.partial(place_kernel, total * slots), out_shape=...]
    pallas_call x1, Pallas kernels: 108 us -> 104 us  [body(): pl.pallas_call(functools.partial(shampoo_kernel, dp, sh, slots), out_shap...]
where the time goes in v2:
time: 113 us
  Pallas kernels  109 us (96%)
  other arithmetic  3.68 us (3%)
    pallas_call x1, Pallas kernels, body(): pl.pallas_call(functools.partial(shampoo_kernel, dp, sh, slots), out_shap...  104 us
    pallas_call x1, Pallas kernels, body(): pl.pallas_call(functools.partial(place_kernel, total * slots), out_shape=...  4.7 us

profile of v2, /device:TPU:9, one launch (start us, length us, event | category | flops | bytes accessed | tf_op | source)
XLA Modules:
  0.0 113.0 jit_solution(7126367216391118740)
XLA Ops:
  0.6 0.9 convert_reduce_fusion
  1.5 1.3 %multiply_add_fusion = (s32[32]{0:T(128)S(1)}, s32[]{:T(128)}, s32[32]{0:T(128)S(1)}) fusion(s32[32]{0:T(128)S(1)} %convert_reduce_fusion, s32[32]{0:T(128)} %param.9, s32[]{:T(128)S(6)} %add.13, s32[32]{0:T(128)} %param.11, s32[32]{0:T(128)} %param.10), kind=kLoop, calls=%fused_computation.19 | loop fusion | flops 1183 | bytes 776 | tf_op jit(solution)/shard_map/add | solution.py:278
  2.9 0.1 select_reduce_fusion
  3.0 0.1 select_reduce_fusion.1
  3.1 1.2 %pad_add_fusion.table_ref = s32[97]{0:T(128)} fusion(s32[1]{0:T(128)} %bitcast, s32[32]{0:T(128)S(1)} %select_reduce_fusion, s32[64]{0:T(128)S(1)} %select_reduce_fusion.1), kind=kLoop, calls=%fused_computation.17 | loop fusion | flops 194 | bytes 776 | tf_op jit(solution)/shard_map/concatenate | solution.py:288
  4.3 0.0 copy-start
  4.3 103.8 %shampoo.1 = (bf16[64,64,128]{2,1,0:T(8,128)(2,1)S(1)}, f32[2,512,512]{2,1,0:T(8,128)S(1)}, f32[2,512,512]{2,1,0:T(8,128)S(1)}, f32[2,512,512]{2,1,0:T(8,128)S(1)}, f32[2,512,512]{2,1,0:T(8,128)S(1)}) custom-call(s32[97]{0:T(128)} %pad_add_fusion.table_ref, bf16[1,2,64,16,512]{4,3,2,1,0:T(8,128)(2,1)} %grad_ref.1, f32[2,512,512]{2,1,0:T(8,128)} %lf_hbm.1, ...), custom_call_target="tpu_custom_call" | custom-call | tf_op jit(solution)/shard_map/shampoo/pallas_call | solution.py:298
  108.2 0.0 copy-done
  108.2 4.7 %place.1 = (bf16[2,64,16,128]{3,2,1,0:T(8,128)(2,1)}, f32[2,512,512]{2,1,0:T(8,128)}, f32[2,512,512]{2,1,0:T(8,128)}, f32[2,512,512]{2,1,0:T(8,128)}, f32[2,512,512]{2,1,0:T(8,128)}) custom-call(s32[97]{0:T(128)S(1)} %copy-done, bf16[64,64,128]{2,1,0:T(8,128)(2,1)S(1)} %get-tuple-element.10.returned, f32[2,512,512]{2,1,0:T(8,128)S(1)} %get-tuple-element.11.refs_0_, ...), custom_call_target="tpu_custom_call" | custom-call | tf_op jit(solution)/shard_map/place/pallas_call | solution.py:324
Async XLA Ops:
  4.3 103.8 %copy-start = (s32[97]{0:T(128)S(1)}, s32[97]{0:T(128)}, u32[]{:S(2)}) copy-start(s32[97]{0:T(128)} %pad_add_fusion.table_ref) | copy-start | bytes 1168

commit v3 on v2

--- a/solution.py
+++ b/solution.py
@@ -41,18 +41,57 @@
     return 1.25 * old_root - mm3(power, split(factor)) * (size / (4.0 * trace))
 
 
-def shampoo_kernel(n, sh, slots, table_ref, grad_ref, lf_hbm, rf_hbm, lr_hbm, rr_hbm,
-                   returned, nlf_ref, nrf_ref, nlr_ref, nrr_ref,
-                   own, from_left, from_right, acc, pieces, packed, g_ref, u_ref,
+def arrivals(n, parts):
+    events = {me: [] for me in range(n)}
+    for step in (1, -1):
+        line = list(range(n))[::step]
+        ready = {(t, b): 0 for t in line[:0:-1] for b in range(parts)}
+        for k, me in enumerate(line[:-1]):
+            free = 0
+            for (t, b), at in sorted(ready.items(), key=lambda item: item[1]):
+                if t in line[:k + 1]:
+                    continue
+                events[me].append((at, t, b, step))
+                free = ready[t, b] = max(free, at) + 1
+    return events
+
+
+def build_table(index, slots, cols, size, owner_ref, row_ref, col_ref, table):
+    blocks = owner_ref.shape[1]
+    square = (blocks, blocks)
+    row = lax.broadcasted_iota(jnp.int32, square, 0)
+    col = lax.broadcasted_iota(jnp.int32, square, 1)
+
+    def upright(x):
+        return jnp.sum(jnp.where(row == col, x, 0), axis=1, keepdims=True)
+
+    def total(pick, x):
+        return jnp.sum(jnp.where(pick, x, 0), axis=0, keepdims=True)
+
+    shift = size.bit_length() - 1
+    owner = owner_ref[...]
+    slot = owner * slots + total((upright(owner) == owner) & (row < col), 1)
+    block = lax.shift_right_logical(row_ref[...], shift) * cols
+    block = block + lax.shift_right_logical(col_ref[...], shift)
+    slot, block = upright(slot), upright(block)
+    lanes = table.shape[1]
+    lane = lax.broadcasted_iota(jnp.int32, (blocks, lanes), 1)
+    table[0:1] = total(slot == lane, block)
+    table[1:2] = total(block == lane, slot)
+    table[2:3] = total(upright(owner) == index, jnp.ones((blocks, lanes), jnp.int32))
+
+
+def shampoo_kernel(n, sh, slots, owner_ref, row_ref, col_ref, grad_ref, lf_hbm, rf_hbm, lr_hbm, rr_hbm,
+                   table, returned, nlf_ref, nrf_ref, nlr_ref, nrr_ref,
+                   own, from_left, from_right, acc, pieces, packed, g_ref, u_ref, table_ref,
                    factors, roots, powers,
-                   load_sem, factor_sem, root_sem, send_sem, left_sem, right_sem,
+                   load_sem, table_sem, factor_sem, root_sem, send_sem, left_sem, right_sem,
                    out_sem, in_sem, back_out_sem, back_in_sem):
     me = lax.axis_index("dp")
     shard = lax.axis_index("shard")
     total = n * sh
     parts, rows, cols, width = own.shape[1:]
     size = g_ref.shape[1]
-    blocks = parts * cols
     index = me * sh + shard
     loads = {}
     order = []
@@ -119,25 +158,35 @@
         own[t, b] = (own[t, b].astype(f32) + buffer[t, b].astype(f32)).astype(bf16)
         hop(t, b, step).start()
 
-    hops = [
-        (t, b, step)
-        for j in range(n - 1)
-        for b in range(parts)
-        for t, step in ((n - 1 - j, 1), (j, -1))
-    ]
-    for t, b, step in hops:
-        pl.when(me == (0 if step > 0 else n - 1))(functools.partial(first_hop, t, b, step))
+    events = arrivals(n, parts)
+    for end in (0, n - 1):
+
+        @pl.when(me == end)
+        def _():
+            for _, t, b, step in events[end]:
+                first_hop(t, b, step)
+
+    build_table(index, slots, cols, size, owner_ref, row_ref, col_ref, table)
+    table_copy = pltpu.make_async_copy(table, table_ref, table_sem)
+    table_copy.start()
     for copy in root_loads:
         copy.wait()
     next_power()
-    every = max(1, 2 * parts // 2)
-    for k, (t, b, step) in enumerate(hops):
-        inner = (me < t) & (me > 0) if step > 0 else (me > t) & (me < n - 1)
-        pl.when(inner)(functools.partial(pass_on, t, b, step))
-        if k % every == every - 1:
-            next_power()
+    last = max(at for k in range(1, n - 1) for at, *_ in events[k])
+    for now in range(1, last + 1):
+        for k in range(1, n - 1):
+            arriving = [event for event in events[k] if event[0] == now]
+            if arriving:
+
+                @pl.when(me == k)
+                def _():
+                    for _, t, b, step in arriving:
+                        pass_on(t, b, step)
+
+        next_power()
     while units:
         next_power()
+    table_copy.wait()
     for copy in factor_loads:
         copy.wait()
     for b in range(parts):
@@ -168,7 +217,7 @@
     def forward(slot):
         @pl.loop(0, total)
         def _(d):
-            packed[slot, d] = pieces[table_ref[d * slots + slot]]
+            packed[slot, d] = pieces[table_ref[0, d * slots + slot]]
 
         def send(z, s):
             pltpu.make_async_remote_copy(
@@ -205,7 +254,7 @@
         ref = packed.at[0, pl.ds(0, total - 1)]
         pltpu.make_async_copy(ref, ref, sem).wait()
 
-    count = table_ref[total * slots + blocks]
+    count = table_ref[2, 0]
     rate = (1.0 - decay_rate) / size
 
     def step(slot):
@@ -243,9 +292,11 @@
                 hop(t, b, 1).wait_send()
 
 
-def place_kernel(first, table_ref, returned, *refs):
+def place_kernel(table, returned, *refs):
     news, out_ref, outs = refs[:4], refs[4], refs[5:9]
-    acc, sems = refs[9:]
+    acc, table_ref, table_sem, sems = refs[9:]
+    table_copy = pltpu.make_async_copy(table, table_ref, table_sem)
+    table_copy.start()
     copies = [
         pltpu.make_async_copy(new, out, sems.at[i])
         for i, (new, out) in enumerate(zip(news, outs))
@@ -253,9 +304,10 @@
     for copy in copies:
         copy.start()
     parts, _, cols, _ = out_ref.shape
+    table_copy.wait()
     for b in range(parts):
         for c in range(cols):
-            acc[b, :, c, :] = returned[table_ref[first + b * cols + c]].astype(f32)
+            acc[b, :, c, :] = returned[table_ref[1, b * cols + c]].astype(f32)
         out_ref[b] = acc[b].astype(bf16)
     for copy in copies:
         copy.wait()
@@ -271,23 +323,9 @@
     width = size // dp
     total = dp * sh
     blocks = owner_list.shape[0]
-    block_at = row_offset // size * cols + col_offset // size
-    entry_index = jnp.arange(blocks, dtype=jnp.int32)
-    same_owner = owner_list[None, :] == owner_list[:, None]
-    earlier = jnp.sum(same_owner & (entry_index[None, :] < entry_index[:, None]), axis=1)
-    slot_of = owner_list * slots + earlier
-    slot_index = jnp.arange(total * slots, dtype=jnp.int32)
-    block_of_slot = jnp.sum(
-        jnp.where(slot_of[None, :] == slot_index[:, None], block_at[None, :], 0), axis=1
-    )
-    slot_of_block = jnp.sum(
-        jnp.where(block_at[None, :] == entry_index[:, None], slot_of[None, :], 0), axis=1
-    )
-    my_index = lax.axis_index(("dp", "shard"))
-    my_count = jnp.sum((owner_list == my_index).astype(jnp.int32), keepdims=True)
-    table = jnp.concatenate([block_of_slot, slot_of_block, my_count]).astype(jnp.int32)
-
-    smem = pl.BlockSpec(memory_space=pltpu.SMEM)
+    lanes = -(-max(total * slots, blocks) // 128) * 128
+    rowed = [x.reshape(1, blocks) for x in (owner_list, row_offset, col_offset)]
+
     vmem = pl.BlockSpec(memory_space=pltpu.VMEM)
     hbm = pl.BlockSpec(memory_space=pltpu.HBM)
     chunk = (dp, parts, rows, cols, width)
@@ -295,11 +333,11 @@
     dma = pltpu.SemaphoreType.DMA
     full = jax.ShapeDtypeStruct(matrices, f32)
     pieces = (total * slots, rows, width)
-    returned, *news = pl.pallas_call(
+    table, returned, *news = pl.pallas_call(
         functools.partial(shampoo_kernel, dp, sh, slots),
-        out_shape=[pltpu.VMEM(pieces, bf16)] + [pltpu.VMEM(matrices, f32)] * 4,
-        in_specs=[smem] + [hbm] * 5,
-        out_specs=[vmem] * 5,
+        out_shape=[pltpu.VMEM((8, lanes), jnp.int32), pltpu.VMEM(pieces, bf16)] + [pltpu.VMEM(matrices, f32)] * 4,
+        in_specs=[vmem] * 3 + [hbm] * 5,
+        out_specs=[vmem] * 6,
         scratch_shapes=[
             pltpu.VMEM(chunk, bf16),
             pltpu.VMEM(chunk, bf16),
@@ -309,10 +347,11 @@
             pltpu.VMEM((slots, total, rows, width), bf16),
             pltpu.VMEM(matrices, bf16),
             pltpu.VMEM(matrices, bf16),
+            pltpu.SMEM((8, lanes), jnp.int32),
             pltpu.VMEM((2,) + matrices, f32),
             pltpu.VMEM((2,) + matrices, f32),
             pltpu.VMEM((2, 2) + matrices, bf16),
-            dma((dp, parts)), dma((2,)), dma((2,)),
+            dma((dp, parts)), dma, dma((2,)), dma((2,)),
             dma((dp, parts)), dma((dp, parts)), dma((dp, parts)),
             dma((slots,)), dma((slots,)), dma((slots,)), dma((slots,)),
         ],
@@ -320,13 +359,17 @@
             collective_id=0, has_side_effects=True, vmem_limit_bytes=48 * 2**20
         ),
         name="shampoo",
-    )(table, gradients, left_factor, right_factor, left_root, right_root)
+    )(*rowed, gradients, left_factor, right_factor, left_root, right_root)
     return pl.pallas_call(
-        functools.partial(place_kernel, total * slots),
+        place_kernel,
         out_shape=[jax.ShapeDtypeStruct((parts, rows, cols, width), bf16)] + [full] * 4,
-        in_specs=[smem] + [vmem] * 5,
+        in_specs=[vmem] * 6,
         out_specs=[vmem] + [hbm] * 4,
-        scratch_shapes=[pltpu.VMEM((parts, rows, cols, width), f32), dma((4,))],
+        scratch_shapes=[
+            pltpu.VMEM((parts, rows, cols, width), f32),
+            pltpu.SMEM((8, lanes), jnp.int32),
+            dma, dma((4,)),
+        ],
         compiler_params=pltpu.CompilerParams(vmem_limit_bytes=16 * 2**20),
         name="place",
     )(table, returned, *news)

time: 113 us -> 92 us (0.81)
  Pallas kernels: 109 us -> 91 us
  other arithmetic: 3.68 us -> 0 us
    pallas_call x1, Pallas kernels: 104 us -> 86.9 us  [body(): pl.pallas_call(functools.partial(shampoo_kernel, dp, sh, slots), out_shap...]
    add x1 -> x0, other arithmetic: 1.33 us -> none  [body(): slot_of = owner_list * slots + earlier]
    concatenate x1 -> x0, other arithmetic: 1.24 us -> none  [body(): jnp.concatenate([block_of_slot, slot_of_block, my_count]).astype(jnp.int32)]
where the time goes in v3:
time: 92 us; the launch traced here: 91.8 us
  Pallas kernels  91 us (99%)
    pallas_call x1, Pallas kernels, body(): pl.pallas_call(functools.partial(shampoo_kernel, dp, sh, slots), out_shap...  86.9 us
    pallas_call x1, Pallas kernels, body(): pl.pallas_call(place_kernel, out_shape=[jax.ShapeDtypeStruct((parts, rows...  4.17 us

profile of v3, /device:TPU:9, one launch (start us, length us, event | category | flops | bytes accessed | tf_op | source)
XLA Modules:
  0.0 91.8 jit_solution(578963186361262228)
XLA Ops:
  0.6 86.9 %shampoo.1 = (s32[8,128]{1,0:T(8,128)S(1)}, bf16[64,64,128]{2,1,0:T(8,128)(2,1)S(1)}, f32[2,512,512]{2,1,0:T(8,128)S(1)}, f32[2,512,512]{2,1,0:T(8,128)S(1)}, f3...) custom-call(s32[1,32]{1,0:T(1,128)} %bitcast.3, s32[1,32]{1,0:T(1,128)} %bitcast.4, s32[1,32]{1,0:T(1,128)} %bitcast.5, ...), custom_call_target="tpu_custom_call" | custom-call | tf_op jit(solution)/shard_map/shampoo/pallas_call | solution.py:336
  87.5 4.2 %place.1 = (bf16[2,64,16,128]{3,2,1,0:T(8,128)(2,1)}, f32[2,512,512]{2,1,0:T(8,128)}, f32[2,512,512]{2,1,0:T(8,128)}, f32[2,512,512]{2,1,0:T(8,128)}, f32[2,512,512]{2,1,0:T(8,128)}) custom-call(s32[8,128]{1,0:T(8,128)S(1)} %get-tuple-element.11.table, bf16[64,64,128]{2,1,0:T(8,128)(2,1)S(1)} %get-tuple-element.12.returned, ...), custom_call_target="tpu_custom_call" | custom-call | tf_op jit(solution)/shard_map/place/pallas_call | solution.py:363

commit v4 on v3

--- a/solution.py
+++ b/solution.py
@@ -26,13 +26,6 @@
     return mm(a[0], b[0]) + (mm(a[0], b[1]) + mm(a[1], b[0]))
 
 
-def fifth_power(x):
-    x = split(x)
-    square = split(mm3(x, x))
-    quad = split(mm3(square, square))
-    return split(mm3(quad, x))
-
-
 def root_of(factor, power, old_root):
     size = factor.shape[0]
     row = lax.broadcasted_iota(jnp.int32, factor.shape, 0)
@@ -41,19 +34,44 @@
     return 1.25 * old_root - mm3(power, split(factor)) * (size / (4.0 * trace))
 
 
-def arrivals(n, parts):
+def share_out(n, rows):
+    tall = 32 if rows % 32 == 0 else rows
+    cells = [(q, r) for q in range(n) for r in range(0, rows, tall)]
+    shares = [len(cells) // n] * n
+    if n == 4 and len(cells) % 8 == 0:
+        shares = [len(cells) * 3 // 8, len(cells) // 8, len(cells) // 8, len(cells) * 3 // 8]
+    starts = [sum(shares[:me]) for me in range(n)]
+    return tall, [cells[at:at + share] for at, share in zip(starts, shares)]
+
+
+def runs_of(cells, tall):
+    runs = []
+    for k, (q, r) in enumerate(cells):
+        if runs and runs[-1][1] == q:
+            runs[-1][3] += tall
+        else:
+            runs.append([k * tall, q, r, tall])
+    return runs
+
+
+def arrivals(owned, parts, latency=0.75):
+    n = len(owned)
     events = {me: [] for me in range(n)}
+    finals = {me: {} for me in range(n)}
     for step in (1, -1):
         line = list(range(n))[::step]
-        ready = {(t, b): 0 for t in line[:0:-1] for b in range(parts)}
-        for k, me in enumerate(line[:-1]):
+        ready = {(q, r, b, t): 0 for t in line[:0:-1] for q, r in owned[t] for b in range(parts)}
+        for me in line:
             free = 0
-            for (t, b), at in sorted(ready.items(), key=lambda item: item[1]):
-                if t in line[:k + 1]:
-                    continue
-                events[me].append((at, t, b, step))
-                free = ready[t, b] = max(free, at) + 1
-    return events
+            for chunk, at in sorted(ready.items(), key=lambda item: item[1]):
+                if chunk[3] == me:
+                    finals[me][chunk] = max(finals[me].get(chunk, 0), at)
+                    del ready[chunk]
+                else:
+                    events[me].append((at, chunk, step))
+                    free = max(free, at) + 1
+                    ready[chunk] = free + latency
+    return events, {me: sorted(finals[me], key=finals[me].get) for me in range(n)}
 
 
 def build_table(index, slots, cols, size, owner_ref, row_ref, col_ref, table):
@@ -92,6 +110,9 @@
     total = n * sh
     parts, rows, cols, width = own.shape[1:]
     size = g_ref.shape[1]
+    tall, owned = share_out(n, rows)
+    events, finals = arrivals(owned, parts)
+    chunks = [(q, r, b, t) for t in range(n) for q, r in owned[t] for b in range(parts)]
     index = me * sh + shard
     loads = {}
     order = []
@@ -129,42 +150,67 @@
             loads[t, b].wait()
     pl.semaphore_wait(barrier, total - 1)
 
-    def hop(t, b, step):
+    def place_of(chunk):
+        q, r, b, _ = chunk
+        return (q, b, pl.ds(r, tall)), (q, r // tall, b)
+
+    def hop(chunk, step):
         buffer, sem = (from_left, left_sem) if step > 0 else (from_right, right_sem)
+        at, sem_at = place_of(chunk)
         return pltpu.make_async_remote_copy(
-            src_ref=own.at[t, b],
-            dst_ref=buffer.at[t, b],
-            send_sem=send_sem.at[t, b],
-            recv_sem=sem.at[t, b],
+            src_ref=own.at[at],
+            dst_ref=buffer.at[at],
+            send_sem=send_sem.at[sem_at],
+            recv_sem=sem.at[sem_at],
             device_id=(me + step, shard),
             device_id_type=MESH,
         )
 
-    units = [(i, s) for s in range(slots) for i in range(2)]
+    units = [(i, s, part) for s in range(slots) for i in range(2) for part in range(3)]
 
     def next_power():
         if units:
-            i, s = units.pop(0)
-            hi, lo = fifth_power(roots[i, s])
-            powers[i, 0, s] = hi
-            powers[i, 1, s] = lo
-
-    def first_hop(t, b, step):
-        hop(t, b, step).start()
-
-    def pass_on(t, b, step):
-        hop(t, b, step).wait_recv()
+            i, s, part = units.pop(0)
+            if part == 0:
+                x = split(roots[i, s])
+                result = mm3(x, x)
+            else:
+                x = (powers[i, 0, s], powers[i, 1, s])
+                result = mm3(x, x if part == 1 else split(roots[i, s]))
+            powers[i, 0, s], powers[i, 1, s] = split(result)
+
+    def pass_on(chunk, step):
+        hop(chunk, step).wait_recv()
         buffer = from_left if step > 0 else from_right
-        own[t, b] = (own[t, b].astype(f32) + buffer[t, b].astype(f32)).astype(bf16)
-        hop(t, b, step).start()
-
-    events = arrivals(n, parts)
+        at, _ = place_of(chunk)
+        own[at] = (own[at].astype(f32) + buffer[at].astype(f32)).astype(bf16)
+        hop(chunk, step).start()
+
+    def finish(k, chunk):
+        at, _ = place_of(chunk)
+        value = own[at].astype(f32)
+        if k > 0:
+            hop(chunk, 1).wait_recv()
+            value = value + from_left[at].astype(f32)
+        if k < n - 1:
+            hop(chunk, -1).wait_recv()
+            value = value + from_right[at].astype(f32)
+        q, r, b, _ = chunk
+        acc[...] = value
+        first = owned[k].index((q, r)) * tall
+        for c in range(cols):
+            pieces[b * cols + c, first:first + tall] = acc[:, c, :].astype(bf16)
+
+    def by_plane(visit):
+        for k in range(n):
+            pl.when(me == k)(functools.partial(visit, k))
+
     for end in (0, n - 1):
 
         @pl.when(me == end)
         def _():
-            for _, t, b, step in events[end]:
-                first_hop(t, b, step)
+            for _, chunk, step in events[end]:
+                hop(chunk, step).start()
 
     build_table(index, slots, cols, size, owner_ref, row_ref, col_ref, table)
     table_copy = pltpu.make_async_copy(table, table_ref, table_sem)
@@ -172,38 +218,31 @@
     for copy in root_loads:
         copy.wait()
     next_power()
-    last = max(at for k in range(1, n - 1) for at, *_ in events[k])
-    for now in range(1, last + 1):
+    next_power()
+    times = sorted({at for k in range(1, n - 1) for at, *_ in events[k]})
+    pace = -(-len(units) // max(1, len(times) - 1))
+    for now in times:
         for k in range(1, n - 1):
             arriving = [event for event in events[k] if event[0] == now]
             if arriving:
 
                 @pl.when(me == k)
                 def _():
-                    for _, t, b, step in arriving:
-                        pass_on(t, b, step)
-
-        next_power()
+                    for _, chunk, step in arriving:
+                        pass_on(chunk, step)
+
+        for _ in range(pace):
+            next_power()
     while units:
         next_power()
     table_copy.wait()
     for copy in factor_loads:
         copy.wait()
-    for b in range(parts):
-        acc[b] = own[me, b].astype(f32)
-
-        @pl.when(me > 0)
-        def _():
-            hop(me, b, 1).wait_recv()
-            acc[b] += from_left[me, b].astype(f32)
-
-        @pl.when(me < n - 1)
-        def _():
-            hop(me, b, -1).wait_recv()
-            acc[b] += from_right[me, b].astype(f32)
-
-        for c in range(cols):
-            pieces[b * cols + c] = acc[b, :, c, :].astype(bf16)
+
+    @by_plane
+    def _(k):
+        for chunk in finals[k]:
+            finish(k, chunk)
 
     my_rows = pl.ds(pl.multiple_of(shard * rows, rows), rows)
     my_cols = pl.ds(pl.multiple_of(me * width, width), width)
@@ -214,23 +253,43 @@
             def _(ds):
                 visit(lax.rem(me + dz, n), lax.rem(shard + ds, sh))
 
-    def forward(slot):
+    def forward(slot, k):
+        tops = len(owned[k]) * tall
+
         @pl.loop(0, total)
         def _(d):
-            packed[slot, d] = pieces[table_ref[0, d * slots + slot]]
+            packed[slot, d, 0:tops] = pieces[table_ref[0, d * slots + slot], 0:tops]
+
+        def block_part(q, r, high):
+            return (
+                slot,
+                pl.ds(pl.multiple_of(shard * rows + r, tall), high),
+                pl.ds(q * width, width),
+            )
 
         def send(z, s):
-            pltpu.make_async_remote_copy(
-                src_ref=packed.at[slot, z * sh + s],
-                dst_ref=g_ref.at[slot, my_rows, my_cols],
-                send_sem=out_sem.at[slot],
-                recv_sem=in_sem.at[slot],
-                device_id=(z, s),
-                device_id_type=MESH,
-            ).start()
+            for top, q, r, high in runs_of(owned[k], tall):
+                pltpu.make_async_remote_copy(
+                    src_ref=packed.at[slot, z * sh + s, pl.ds(top, high)],
+                    dst_ref=g_ref.at[block_part(q, r, high)],
+                    send_sem=out_sem.at[slot],
+                    recv_sem=in_sem.at[slot],
+                    device_id=(z, s),
+                    device_id_type=MESH,
+                ).start()
 
         peers(send)
-        g_ref[slot, my_rows, my_cols] = packed[slot, index]
+        for top, q, r, high in runs_of(owned[k], tall):
+            g_ref[block_part(q, r, high)] = packed[slot, index, pl.ds(top, high)]
+
+    def wait_forward(slot, k):
+        incoming = n * (size // tall) - len(owned[k])
+        ref = returned.at[pl.ds(0, incoming), pl.ds(0, tall)]
+        pltpu.make_async_copy(ref, ref, in_sem.at[slot]).wait()
+
+    def wait_forward_sent(slot, k):
+        ref = packed.at[slot, pl.ds(0, total - 1), pl.ds(0, len(owned[k]) * tall)]
+        pltpu.make_async_copy(ref, ref, out_sem.at[slot]).wait()
 
     def backward(slot):
         def send(z, s):
@@ -250,8 +309,8 @@
         peers(send)
         returned[index * slots + slot] = u_ref[slot, my_rows, my_cols]
 
-    def wait_all(sem):
-        ref = packed.at[0, pl.ds(0, total - 1)]
+    def wait_return(sem):
+        ref = returned.at[pl.ds(0, total - 1)]
         pltpu.make_async_copy(ref, ref, sem).wait()
 
     count = table_ref[2, 0]
@@ -273,23 +332,24 @@
         product = split(mm(hi, g) + mm(lo, g))
         u_ref[slot] = mm3(product, split(right_root)).astype(bf16)
 
+    @by_plane
+    def _(k):
+        for slot in range(slots):
+            forward(slot, k)
+
     for slot in range(slots):
-        forward(slot)
-    for slot in range(slots):
-        wait_all(in_sem.at[slot])
+        by_plane(functools.partial(wait_forward, slot))
         step(slot)
         backward(slot)
     for slot in range(slots):
-        wait_all(back_in_sem.at[slot])
-    for slot in range(slots):
-        wait_all(out_sem.at[slot])
-        wait_all(back_out_sem.at[slot])
-    for t in range(n):
-        for b in range(parts):
-
-            @pl.when(me != t)
-            def _():
-                hop(t, b, 1).wait_send()
+        wait_return(back_in_sem.at[slot])
+        wait_return(back_out_sem.at[slot])
+        by_plane(functools.partial(wait_forward_sent, slot))
+    for chunk in chunks:
+
+        @pl.when(me != chunk[3])
+        def _():
+            hop(chunk, 1).wait_send()
 
 
 def place_kernel(table, returned, *refs):
@@ -323,6 +383,9 @@
     width = size // dp
     total = dp * sh
     blocks = owner_list.shape[0]
+    tall, owned = share_out(dp, rows)
+    held = max(len(cells) for cells in owned) * tall
+    hops = (dp, rows // tall, parts)
     lanes = -(-max(total * slots, blocks) // 128) * 128
     rowed = [x.reshape(1, blocks) for x in (owner_list, row_offset, col_offset)]
 
@@ -342,9 +405,9 @@
             pltpu.VMEM(chunk, bf16),
             pltpu.VMEM(chunk, bf16),
             pltpu.VMEM(chunk, bf16),
-            pltpu.VMEM(chunk[1:], f32),
-            pltpu.VMEM((parts * cols, rows, width), bf16),
-            pltpu.VMEM((slots, total, rows, width), bf16),
+            pltpu.VMEM((tall, cols, width), f32),
+            pltpu.VMEM((parts * cols, held, width), bf16),
+            pltpu.VMEM((slots, total, held, width), bf16),
             pltpu.VMEM(matrices, bf16),
             pltpu.VMEM(matrices, bf16),
             pltpu.SMEM((8, lanes), jnp.int32),
@@ -352,7 +415,7 @@
             pltpu.VMEM((2,) + matrices, f32),
             pltpu.VMEM((2, 2) + matrices, bf16),
             dma((dp, parts)), dma, dma((2,)), dma((2,)),
-            dma((dp, parts)), dma((dp, parts)), dma((dp, parts)),
+            dma(hops), dma(hops), dma(hops),
             dma((slots,)), dma((slots,)), dma((slots,)), dma((slots,)),
         ],
         compiler_params=pltpu.CompilerParams(

time: 92 us -> 87 us (0.946)
  Pallas kernels: 91 us -> 85.6 us
    pallas_call x1, Pallas kernels: 86.9 us -> 81.4 us  [body(): pl.pallas_call(functools.partial(shampoo_kernel, dp, sh, slots), out_shap...]
where the time goes in v4:
time: 87 us; the launch traced here: 86.4 us
  Pallas kernels  85.6 us (98%)
    pallas_call x1, Pallas kernels, body(): pl.pallas_call(functools.partial(shampoo_kernel, dp, sh, slots), out_shap...  81.4 us
    pallas_call x1, Pallas kernels, body(): pl.pallas_call(place_kernel, out_shape=[jax.ShapeDtypeStruct((parts, rows...  4.17 us

profile of v4, /device:TPU:9, one launch (start us, length us, event | category | flops | bytes accessed | tf_op | source)
XLA Modules:
  0.0 86.4 jit_solution(2179665219452107228)
XLA Ops:
  0.6 81.4 %shampoo.1 = (s32[8,128]{1,0:T(8,128)S(1)}, bf16[64,64,128]{2,1,0:T(8,128)(2,1)S(1)}, f32[2,512,512]{2,1,0:T(8,128)S(1)}, f32[2,512,512]{2,1,0:T(8,128)S(1)}, f3...) custom-call(s32[1,32]{1,0:T(1,128)} %bitcast.3, s32[1,32]{1,0:T(1,128)} %bitcast.4, s32[1,32]{1,0:T(1,128)} %bitcast.5, ...), custom_call_target="tpu_custom_call" | custom-call | tf_op jit(solution)/shard_map/shampoo/pallas_call | solution.py:399
  82.1 4.2 %place.1 = (bf16[2,64,16,128]{3,2,1,0:T(8,128)(2,1)}, f32[2,512,512]{2,1,0:T(8,128)}, f32[2,512,512]{2,1,0:T(8,128)}, f32[2,512,512]{2,1,0:T(8,128)}, f32[2,512,512]{2,1,0:T(8,128)}) custom-call(s32[8,128]{1,0:T(8,128)S(1)} %get-tuple-element.11.table, bf16[64,64,128]{2,1,0:T(8,128)(2,1)S(1)} %get-tuple-element.12.returned, ...), custom_call_target="tpu_custom_call" | custom-call | tf_op jit(solution)/shard_map/place/pallas_call | solution.py:426

commit v5 on v4

--- a/solution.py
+++ b/solution.py
@@ -114,6 +114,15 @@
     events, finals = arrivals(owned, parts)
     chunks = [(q, r, b, t) for t in range(n) for q, r in owned[t] for b in range(parts)]
     index = me * sh + shard
+    barrier = pltpu.get_barrier_semaphore()
+
+    @pl.loop(1, total)
+    def _(r):
+        to = lax.rem(index + r, total)
+        pl.semaphore_signal(
+            barrier, inc=1, device_id=(to // sh, lax.rem(to, sh)), device_id_type=MESH
+        )
+
     loads = {}
     order = []
     for j in range(n):
@@ -136,15 +145,6 @@
     ]
     for copy in root_loads + factor_loads:
         copy.start()
-    barrier = pltpu.get_barrier_semaphore()
-
-    @pl.loop(1, total)
-    def _(r):
-        to = lax.rem(index + r, total)
-        pl.semaphore_signal(
-            barrier, inc=1, device_id=(to // sh, lax.rem(to, sh)), device_id_type=MESH
-        )
-
     for t in order:
         for b in range(parts):
             loads[t, b].wait()
@@ -247,18 +247,22 @@
     my_rows = pl.ds(pl.multiple_of(shard * rows, rows), rows)
     my_cols = pl.ds(pl.multiple_of(me * width, width), width)
 
-    def peers(visit):
-        for dz in sorted(range(n), key=lambda d: abs(2 * d - n)):
-            @pl.loop(0 if dz else 1, sh)
-            def _(ds):
-                visit(lax.rem(me + dz, n), lax.rem(shard + ds, sh))
+    def planes_from(k):
+        return sorted(range(n), key=lambda z: ((2 * z < n) == (2 * k < n), -abs(z - k)))
+
+    def peers(k, z, visit):
+        @pl.loop(1 if z == k else 0, sh)
+        def _(ds):
+            visit(z, lax.rem(shard + ds, sh))
 
     def forward(slot, k):
         tops = len(owned[k]) * tall
 
-        @pl.loop(0, total)
-        def _(d):
-            packed[slot, d, 0:tops] = pieces[table_ref[0, d * slots + slot], 0:tops]
+        def pack(z):
+            @pl.loop(0, sh)
+            def _(s):
+                d = z * sh + s
+                packed[slot, d, 0:tops] = pieces[table_ref[0, d * slots + slot], 0:tops]
 
         def block_part(q, r, high):
             return (
@@ -278,7 +282,12 @@
                     device_id_type=MESH,
                 ).start()
 
-        peers(send)
+        planes = planes_from(k)
+        pack(planes[0])
+        for z, following in zip(planes, planes[1:] + [None]):
+            if following is not None:
+                pack(following)
+            peers(k, z, send)
         for top, q, r, high in runs_of(owned[k], tall):
             g_ref[block_part(q, r, high)] = packed[slot, index, pl.ds(top, high)]
 
@@ -291,7 +300,7 @@
         ref = packed.at[slot, pl.ds(0, total - 1), pl.ds(0, len(owned[k]) * tall)]
         pltpu.make_async_copy(ref, ref, out_sem.at[slot]).wait()
 
-    def backward(slot):
+    def backward(slot, k):
         def send(z, s):
             pltpu.make_async_remote_copy(
                 src_ref=u_ref.at[
@@ -306,7 +315,8 @@
                 device_id_type=MESH,
             ).start()
 
-        peers(send)
+        for z in planes_from(k):
+            peers(k, z, send)
         returned[index * slots + slot] = u_ref[slot, my_rows, my_cols]
 
     def wait_return(sem):
@@ -340,7 +350,7 @@
     for slot in range(slots):
         by_plane(functools.partial(wait_forward, slot))
         step(slot)
-        backward(slot)
+        by_plane(functools.partial(backward, slot))
     for slot in range(slots):
         wait_return(back_in_sem.at[slot])
         wait_return(back_out_sem.at[slot])
@@ -354,7 +364,7 @@
 
 def place_kernel(table, returned, *refs):
     news, out_ref, outs = refs[:4], refs[4], refs[5:9]
-    acc, table_ref, table_sem, sems = refs[9:]
+    acc, placed, table_ref, table_sem, sems, out_sem = refs[9:]
     table_copy = pltpu.make_async_copy(table, table_ref, table_sem)
     table_copy.start()
     copies = [
@@ -368,7 +378,9 @@
     for b in range(parts):
         for c in range(cols):
             acc[b, :, c, :] = returned[table_ref[1, b * cols + c]].astype(f32)
-        out_ref[b] = acc[b].astype(bf16)
+        placed[b] = acc[b].astype(bf16)
+        copies.append(pltpu.make_async_copy(placed.at[b], out_ref.at[b], out_sem.at[b]))
+        copies[-1].start()
     for copy in copies:
         copy.wait()
 
@@ -427,11 +439,12 @@
         place_kernel,
         out_shape=[jax.ShapeDtypeStruct((parts, rows, cols, width), bf16)] + [full] * 4,
         in_specs=[vmem] * 6,
-        out_specs=[vmem] + [hbm] * 4,
+        out_specs=[hbm] * 5,
         scratch_shapes=[
             pltpu.VMEM((parts, rows, cols, width), f32),
+            pltpu.VMEM((parts, rows, cols, width), bf16),
             pltpu.SMEM((8, lanes), jnp.int32),
-            dma, dma((4,)),
+            dma, dma((4,)), dma((parts,)),
         ],
         compiler_params=pltpu.CompilerParams(vmem_limit_bytes=16 * 2**20),
         name="place",

time: 87 us -> 86.2 us (level)
  no operation moved by 1% of the time
where the time goes in v5:
time: 86.2 us; the launch traced here: 86 us
  Pallas kernels  85.2 us (99%)
    pallas_call x1, Pallas kernels, body(): pl.pallas_call(functools.partial(shampoo_kernel, dp, sh, slots), out_shap...  81.7 us
    pallas_call x1, Pallas kernels, body(): pl.pallas_call(place_kernel, out_shape=[jax.ShapeDtypeStruct((parts, rows...  3.49 us

profile of v5, /device:TPU:9, one launch (start us, length us, event | category | flops | bytes accessed | tf_op | source)
XLA Modules:
  0.0 86.0 jit_solution(3518017781595177956)
XLA Ops:
  0.6 81.7 %shampoo.1 = (s32[8,128]{1,0:T(8,128)S(1)}, bf16[64,64,128]{2,1,0:T(8,128)(2,1)S(1)}, f32[2,512,512]{2,1,0:T(8,128)S(1)}, f32[2,512,512]{2,1,0:T(8,128)S(1)}, f3...) custom-call(s32[1,32]{1,0:T(1,128)} %bitcast.3, s32[1,32]{1,0:T(1,128)} %bitcast.4, s32[1,32]{1,0:T(1,128)} %bitcast.5, ...), custom_call_target="tpu_custom_call" | custom-call | tf_op jit(solution)/shard_map/shampoo/pallas_call | solution.py:411
  82.4 3.5 %place.1 = (bf16[2,64,16,128]{3,2,1,0:T(8,128)(2,1)}, f32[2,512,512]{2,1,0:T(8,128)}, f32[2,512,512]{2,1,0:T(8,128)}, f32[2,512,512]{2,1,0:T(8,128)}, f32[2,512,512]{2,1,0:T(8,128)}) custom-call(s32[8,128]{1,0:T(8,128)S(1)} %get-tuple-element.11.table, bf16[64,64,128]{2,1,0:T(8,128)(2,1)S(1)} %get-tuple-element.12.returned, ...), custom_call_target="tpu_custom_call" | custom-call | tf_op jit(solution)/shard_map/place/pallas_call | solution.py:438

commit v6 on v5

--- a/solution.py
+++ b/solution.py
@@ -116,11 +116,18 @@
     index = me * sh + shard
     barrier = pltpu.get_barrier_semaphore()
 
-    @pl.loop(1, total)
-    def _(r):
-        to = lax.rem(index + r, total)
+    @pl.when(me > 0)
+    def _():
+        pl.semaphore_signal(barrier, inc=1, device_id=(me - 1, shard), device_id_type=MESH)
+
+    @pl.when(me < n - 1)
+    def _():
+        pl.semaphore_signal(barrier, inc=1, device_id=(me + 1, shard), device_id_type=MESH)
+
+    @pl.loop(1, sh)
+    def _(ds):
         pl.semaphore_signal(
-            barrier, inc=1, device_id=(to // sh, lax.rem(to, sh)), device_id_type=MESH
+            barrier, inc=1, device_id=(me, lax.rem(shard + ds, sh)), device_id_type=MESH
         )
 
     loads = {}
@@ -148,7 +155,8 @@
     for t in order:
         for b in range(parts):
             loads[t, b].wait()
-    pl.semaphore_wait(barrier, total - 1)
+    beside = (me > 0).astype(jnp.int32) + (me < n - 1).astype(jnp.int32)
+    pl.semaphore_wait(barrier, sh - 1 + beside)
 
     def place_of(chunk):
         q, r, b, _ = chunk

time: 86.2 us -> 86 us (level)
  no operation moved by 1% of the time
where the time goes in v6:
time: 86 us; the launch traced here: 85.8 us
  Pallas kernels  85 us (99%)
    pallas_call x1, Pallas kernels, body(): pl.pallas_call(functools.partial(shampoo_kernel, dp, sh, slots), out_shap...  81.6 us
    pallas_call x1, Pallas kernels, body(): pl.pallas_call(place_kernel, out_shape=[jax.ShapeDtypeStruct((parts, rows...  3.49 us

profile of v6, /device:TPU:9, one launch (start us, length us, event | category | flops | bytes accessed | tf_op | source)
XLA Modules:
  0.0 85.8 jit_solution(10370665413709491350)
XLA Ops:
  0.6 81.6 %shampoo.1 = (s32[8,128]{1,0:T(8,128)S(1)}, bf16[64,64,128]{2,1,0:T(8,128)(2,1)S(1)}, f32[2,512,512]{2,1,0:T(8,128)S(1)}, f32[2,512,512]{2,1,0:T(8,128)S(1)}, f3...) custom-call(s32[1,32]{1,0:T(1,128)} %bitcast.3, s32[1,32]{1,0:T(1,128)} %bitcast.4, s32[1,32]{1,0:T(1,128)} %bitcast.5, ...), custom_call_target="tpu_custom_call" | custom-call | tf_op jit(solution)/shard_map/shampoo/pallas_call | solution.py:419
  82.2 3.5 %place.1 = (bf16[2,64,16,128]{3,2,1,0:T(8,128)(2,1)}, f32[2,512,512]{2,1,0:T(8,128)}, f32[2,512,512]{2,1,0:T(8,128)}, f32[2,512,512]{2,1,0:T(8,128)}, f32[2,512,512]{2,1,0:T(8,128)}) custom-call(s32[8,128]{1,0:T(8,128)S(1)} %get-tuple-element.11.table, bf16[64,64,128]{2,1,0:T(8,128)(2,1)S(1)} %get-tuple-element.12.returned, ...), custom_call_target="tpu_custom_call" | custom-call | tf_op jit(solution)/shard_map/place/pallas_call | solution.py:446
